TPU v7x, 256 devices: a whole 4x4x8 slice. The times are simulated.
256 devices in a mesh: subj: 16 (over y_hi, z), slab: 16 (over x, y_lo, core).
Axes of the slice: x: 4, y: 4 (y_hi: 2, y_lo: 2; y = y_hi * 2 + y_lo), z: 8, core: 2. Of those that a mesh axis runs over, the one named last changes fastest.
Arguments:
- fod: bfloat16 [64, 45, 8192], P('subj', None, 'slab'), may hold values from -24 to 24
- rotation: bfloat16 [64, 45, 45, 8192], P('subj', None, None, 'slab'), may hold values from -0.875 to 0.875
- modulation: float32 [64, 8192], P('subj', 'slab'), may hold values from 0.3 to 3
- subject_ids: int32 [64], P('subj'), may hold values from 0 to 63, each once
- subject_weight: float32 [64], replicated, may hold values from 0.5 to 2
- voxel_cell_index: int32 [8192], P('slab'), may hold values from 0 to 1023, as said below
Outputs:
- template: bfloat16 [45, 16384], replicated
Inputs may be any that keep to these rules, and one draw needn't show every extreme that they name: `voxel_cell_index`: within each aligned block of 512 entries (one slab's masked voxels) the cell numbers are distinct and increasing.
All inputs are finite; a program needn't handle non-finite values.
Results may differ from a plain program's by a relative error of at most 0.001.
Values may be sent and summed in bfloat16 or wider, within the bound.
A program may use at most 64 MiB of HBM per device.

v0:
```python
import jax
import jax.numpy as jnp
from jax import lax
from jax.sharding import PartitionSpec as P

GRID_DEV = 1024


def cut_along(value, dim, length):
    lengths = value.shape
    blocks = value.reshape(*lengths[:dim], length, lengths[dim] // length, *lengths[dim + 1 :])
    return jnp.moveaxis(blocks, dim, 0)


def sum_at_owner(value, axis, dim):
    blocks = cut_along(value, dim, lax.axis_size(axis))
    arrived = lax.all_to_all(blocks, axis, split_axis=0, concat_axis=0, tiled=True)
    return arrived.sum(axis=0)


def from_everyone(value, axis):
    copies = jnp.broadcast_to(value, (lax.axis_size(axis), *value.shape))
    return lax.all_to_all(copies, axis, split_axis=0, concat_axis=0, tiled=True)


def laid_out(blocks, dim):
    lengths = list(blocks.shape[1:])
    lengths[dim] *= blocks.shape[0]
    return jnp.moveaxis(blocks, 0, dim).reshape(lengths)


def gather_directly(value, axis, dim):
    blocks = from_everyone(value, axis)
    return laid_out(blocks, dim)


def on_device(fod, rotation, modulation, subject_ids, subject_weight, voxel_cell_index):
    total_subjects = subject_weight.shape[0]
    indicator_rows = (
        subject_ids[:, None] == jnp.arange(total_subjects, dtype=jnp.int32)[None, :]
    ).astype(jnp.float32)
    selected_cells = jnp.dot(indicator_rows, subject_weight, precision=lax.Precision.HIGHEST)
    weight = modulation * selected_cells[:, None]
    rotated_coefficients = jnp.einsum(
        "xfhu,xhu->xfu", rotation, fod, preferred_element_type=jnp.float32
    )
    numer = jnp.sum(rotated_coefficients * weight[:, None, :], axis=0)
    denom = jnp.sum(weight, axis=0)
    numer_share, denom_share = (sum_at_owner(numer, "subj", 1), sum_at_owner(denom, "subj", 0))
    share = (numer_share / denom_share[None, :]).astype(jnp.bfloat16)
    average = gather_directly(share, "subj", 1)
    dense = jnp.zeros((average.shape[0], GRID_DEV), jnp.bfloat16)
    dense = dense.at[:, voxel_cell_index].set(average)
    return gather_directly(dense, "slab", 1)


def solution(mesh):
    placed = (
        P("subj", None, "slab"),
        P("subj", None, None, "slab"),
        P("subj", "slab"),
        P("subj"),
        P(),
        P("slab"),
    )
    return jax.shard_map(on_device, mesh=mesh, in_specs=placed, out_specs=P(), check_vma=False)
```

profile of v0, /device:TPU:1, one launch (start us, length us, event | category | flops | bytes accessed | tf_op | source)
XLA Modules:
  0.0 92.5 jit_solution(17903178454776420858)
XLA Ops:
  0.0 0.7 copy-done
  0.7 0.9 convolution_bitcast_fusion
  1.5 0.8 fusion.4
  2.3 0.7 all_to_all.16
  3.0 11.7 %all-to-all-start.1 = ((f32[16,1,32]{2,1,0:T(1,128)}), f32[16,1,32]{2,1,0:T(1,128)S(1)}, u32[]{:S(2)}, u32[]{:S(2)}) async-start(f32[16,1,32]{2,1,0:T(1,128)} %all_to_all.16), calls=%async_computation.1 | async-start | bytes 16384 | tf_op jit(solution)/shard_map/all_to_all | solution.py:17
  14.7 1.0 %bitcast_convert_fusion = f32[4,512,45]{1,0,2:T(4,128)S(1)} fusion(bf16[4,45,512]{2,0,1:T(4,128)(2,1)} %param.6), kind=kLoop, calls=%fused_computation.4 | loop fusion | flops 92160 | bytes 552960
  15.7 7.8 %multiply_reduce_fusion = f32[4,512,45]{1,0,2:T(4,128)S(1)} fusion(f32[4,512,45]{1,0,2:T(4,128)S(1)} %bitcast_convert_fusion, bf16[4,45,45,512]{3,0,2,1:T(4,128)(2,1)} %param.7), kind=kLoop, calls=%fused_computation.1 | loop fusion | flops 12349440 | bytes 9031680 | tf_op jit(solution)/shard_map/xfhu,xhu->xfu/dot_general | solution.py:44
  23.5 0.2 multiply_reduce_fusion.1
  23.9 0.2 copy.17
  24.1 1.0 %reshape.35 = f32[16,1,1440]{2,1,0:T(1,128)} reshape(f32[16,32,45]{2,1,0:T(8,128)S(1)} %bitcast.31) | data formatting | bytes 184320
  25.1 9.1 %all-to-all-start = ((f32[16,1,1440]{2,1,0:T(1,128)}), f32[16,1,1440]{2,1,0:T(1,128)S(1)}, u32[]{:S(2)}, u32[]{:S(2)}) async-start(f32[16,1,1440]{2,1,0:T(1,128)} %reshape.35), calls=%async_computation | async-start | bytes 196608 | tf_op jit(solution)/shard_map/all_to_all | solution.py:17
  34.2 8.9 %all-to-all-done = f32[16,1,1440]{2,1,0:T(1,128)S(1)} async-done(((f32[16,1,1440]{2,1,0:T(1,128)}), f32[16,1,1440]{2,1,0:T(1,128)S(1)}, u32[]{:S(2)}, u32[]{:S(2)}) %all-to-all-start) | async-done | bytes 92192 | tf_op jit(solution)/shard_map/all_to_all | solution.py:17
  43.1 0.5 broadcast.6
  43.6 0.9 reduce.4
  44.5 0.3 reshape.36
  44.9 0.8 reshape.37
  45.8 3.5 %all-to-all-start.2 = ((bf16[16,2,720]{2,1,0:T(2,128)(2,1)}), bf16[16,2,720]{2,1,0:T(2,128)(2,1)S(1)}, u32[]{:S(2)}, u32[]{:S(2)}) async-start(bf16[16,2,720]{2,1,0:T(2,128)(2,1)} %reshape.37), calls=%async_computation.2 | async-start | bytes 98304 | tf_op jit(solution)/shard_map/all_to_all | solution.py:23
  49.3 8.8 %all-to-all-done.2 = bf16[16,2,720]{2,1,0:T(2,128)(2,1)S(1)} async-done(((bf16[16,2,720]{2,1,0:T(2,128)(2,1)}), bf16[16,2,720]{2,1,0:T(2,128)(2,1)S(1)}, u32[]{:S(2)}, u32[]{:S(2)}) %all-to-all-start.2) | async-done | bytes 46112 | tf_op jit(solution)/shard_map/all_to_all | solution.py:23
  58.1 0.2 reshape.38
  58.3 1.8 %scatter_custom_fusion = bf16[45,1024]{0,1:T(8,128)(2,1)S(1)} fusion(s32[512]{0:T(512)S(1)} %compare_select_fusion, bf16[512,45]{1,0:T(8,128)(2,1)S(1)} %bitcast.33, bf16[]{:T(256)} %constant.0.clone.1), kind=kCustom, calls=%fused_computation.5 | custom fusion | bytes 92162 | tf_op jit(solution)/shard_map/scatter | solution.py:53
  60.5 29.0 %all_to_all.24 = bf16[16,45,1024]{2,1,0:T(8,128)(2,1)S(1)} all-to-all(bf16[16,45,1024]{2,1,0:T(8,128)(2,1)S(1)} %broadcast_in_dim.20), channel_id=1, replica_groups=mesh['subj'=16,'slab'=16] {'slab'}, dimensions={0} | all-to-all | bytes 2949120 | tf_op jit(solution)/shard_map/all_to_all | solution.py:23
  89.5 0.8 copy.20
  90.3 0.2 pad
  90.5 2.0 %copy.29 = bf16[6,8,16,1024]{3,1,2,0:T(8,128)(2,1)} copy(bf16[6,8,16,1024]{3,2,1,0:T(8,128)(2,1)S(1)} %bitcast.28) | data formatting | bytes 3145728
  (12 shorter events, 0.6 us)
Async XLA Ops:
  0.0 0.7 copy-start
  0.7 48.6 %copy-start.1 = (s32[512]{0:T(512)S(1)}, s32[512]{0:T(512)}, u32[]{:S(2)}) copy-start(s32[512]{0:T(512)} %param.11) | copy-start | bytes 6148
  3.0 22.1 %all-to-all-start.1 = ((f32[16,1,32]{2,1,0:T(1,128)}), f32[16,1,32]{2,1,0:T(1,128)S(1)}, u32[]{:S(2)}, u32[]{:S(2)}) async-start(f32[16,1,32]{2,1,0:T(1,128)} %all_to_all.16), calls=%async_computation.1 | async-start | bytes 16384 | tf_op jit(solution)/shard_map/all_to_all | solution.py:17
  25.1 18.0 %all-to-all-start = ((f32[16,1,1440]{2,1,0:T(1,128)}), f32[16,1,1440]{2,1,0:T(1,128)S(1)}, u32[]{:S(2)}, u32[]{:S(2)}) async-start(f32[16,1,1440]{2,1,0:T(1,128)} %reshape.35), calls=%async_computation | async-start | bytes 196608 | tf_op jit(solution)/shard_map/all_to_all | solution.py:17
  45.8 12.3 %all-to-all-start.2 = ((bf16[16,2,720]{2,1,0:T(2,128)(2,1)}), bf16[16,2,720]{2,1,0:T(2,128)(2,1)S(1)}, u32[]{:S(2)}, u32[]{:S(2)}) async-start(bf16[16,2,720]{2,1,0:T(2,128)(2,1)} %reshape.37), calls=%async_computation.2 | async-start | bytes 98304 | tf_op jit(solution)/shard_map/all_to_all | solution.py:23
where the time goes:
time: 93 us; the launch traced here: 92.5 us
  blocking collectives  29 us (31%)
  starting transfers between devices  24.3 us (26%)
  waiting for transfers between devices  17.7 us (19%)
  other arithmetic  10.8 us (12%)
  local copies, waits for them, and re-layouts  9.83 us (11%)
    all_to_all x1, blocking collectives, from_everyone(): return lax.all_to_all(copies, axis, split_axis=0, concat_axis=0, tiled=True)  29 us
    all_to_all x2, starting transfers between devices, sum_at_owner(): lax.all_to_all(blocks, axis, split_axis=0, concat_axis=0, tiled=True)  20.8 us
    all_to_all x2, waiting for transfers between devices, sum_at_owner(): lax.all_to_all(blocks, axis, split_axis=0, concat_axis=0, tiled=True)  8.89 us
    all_to_all x1, waiting for transfers between devices, from_everyone(): return lax.all_to_all(copies, axis, split_axis=0, concat_axis=0, tiled=True)  8.81 us
    dot_general x1, other arithmetic, on_device(): jnp.einsum('xfhu,xhu->xfu', rotation, fod, preferred_element_type=jnp.flo...  7.78 us
    unnamed x11, local copies, waits for them, and re-layouts  5.26 us
    all_to_all x1, starting transfers between devices, from_everyone(): return lax.all_to_all(copies, axis, split_axis=0, concat_axis=0, tiled=True)  3.5 us
    scatter x2, local copies, waits for them, and re-layouts, on_device(): dense = dense.at[:, voxel_cell_index].set(average)  1.99 us
  transfers between devices with their start and end apart: 3, of which 2 were waited for; matrix products, arithmetic and copies ran while one was open for 11% of the time, Pallas kernels for 0%

commit v1 on v0

v1 whole, which is shorter than its diff:
```python
import functools
import jax
import jax.numpy as jnp
from jax import lax
from jax.experimental import pallas as pl
from jax.experimental.pallas import tpu as pltpu
from jax.sharding import PartitionSpec as P

COEF = 45
SUBJ_DEV = 4
LANES = 128
QUARTERS = 4
BLOCKS = 8
GROUPS = 3
OWNERS = GROUPS * QUARTERS
CHUNK = 8
MESH = pl.DeviceIdType.MESH


def cell_map(cells):
    voxels = cells.shape[1]
    high = cells // LANES
    low = cells - high * LANES
    row = lax.broadcasted_iota(jnp.int32, (BLOCKS, voxels), 0)
    lane = lax.broadcasted_iota(jnp.int32, (LANES, voxels), 0)
    one, zero = jnp.float32(1), jnp.float32(0)
    here = jnp.where(high == row, one, zero)
    before = jnp.where(high < row, one, zero)
    less = jnp.where(low < lane, one, zero)
    same = jnp.where(low == lane, one, zero)
    nt = (((1,), (1,)), ((), ()))
    bf = jnp.bfloat16
    rank = lax.dot_general(here.astype(bf), less.astype(bf), nt, preferred_element_type=jnp.float32)
    mask = lax.dot_general(here.astype(bf), same.astype(bf), nt, preferred_element_type=jnp.float32)
    rank = rank + jnp.sum(before, axis=1, keepdims=True)
    return jnp.where(mask > 0.5, rank, -1.0).astype(jnp.int32)


def kernel(n_subj, n_slab, rot_hbm, fod_hbm, mod_hbm, cells_hbm, ids_ref, sw_ref, out_ref,
           rot, fod_b, fod, mod, cells, prod, sums, got, den, slabs, maps,
           rot_sem, in_sem, rs_send, rs_recv, dn_send, dn_recv, ag_send, ag_recv,
           sl_send, sl_recv, sib_send, sib_recv, mp_send, mp_recv):
    me = lax.axis_index("subj")
    slab = lax.axis_index("slab")
    sib = slab + 1 - 2 * lax.rem(slab, 2)
    core = lax.rem(slab, 2)

    ins = [
        pltpu.make_async_copy(mod_hbm, mod, in_sem.at[0]),
        pltpu.make_async_copy(fod_hbm, fod_b, in_sem.at[1]),
        pltpu.make_async_copy(cells_hbm, cells, in_sem.at[2]),
    ]
    for c in ins:
        c.start()
    chunks = []
    for i, c0 in enumerate(range(0, COEF, CHUNK)):
        n = min(CHUNK, COEF - c0)
        cp = pltpu.make_async_copy(rot_hbm.at[pl.ds(c0, n)], rot.at[pl.ds(c0, n)], rot_sem.at[i])
        cp.start()
        chunks.append((c0, n, cp))

    barrier = pltpu.get_barrier_semaphore()

    def greet(k, _):
        pl.semaphore_signal(barrier, inc=1, device_id=(lax.rem(me + k, n_subj), slab), device_id_type=MESH)
        return 0

    lax.fori_loop(1, n_subj, greet, 0)

    def greet_slab(k, _):
        pl.semaphore_signal(barrier, inc=1, device_id=(me, lax.rem(slab + k, n_slab)), device_id_type=MESH)
        return 0

    lax.fori_loop(1, n_slab, greet_slab, 0)

    ins[0].wait()
    row = lax.rem(lax.broadcasted_iota(jnp.int32, (16, LANES), 0), SUBJ_DEV)
    scale = jnp.full((16, LANES), sw_ref[ids_ref[0]], jnp.float32)
    for s in range(1, SUBJ_DEV):
        scale = jnp.where(row == s, sw_ref[ids_ref[s]], scale)
    mod[...] = mod[...] * scale
    parts = [mod[pl.ds(s, QUARTERS, stride=SUBJ_DEV), :] for s in range(SUBJ_DEV)]
    den[me] = (parts[0] + parts[1]) + (parts[2] + parts[3])

    ins[2].wait()
    maps[slab] = cell_map(cells[...])

    ins[1].wait()
    fod[...] = fod_b[...].astype(jnp.float32)

    def compute(c0, n):
        def step(k, acc):
            f = fod[k]
            return tuple(acc[i] + rot[c0 + i, k].astype(jnp.float32) * f for i in range(n))

        acc = lax.fori_loop(0, COEF, step, tuple(jnp.zeros((16, LANES), jnp.float32) for _ in range(n)), unroll=9)
        w = mod[...]
        for i in range(n):
            y = acc[i] * w
            prod[0, pl.ds((c0 + i) * 8, 8), :] = y[:8]
            prod[1, pl.ds((c0 + i) * 8, 8), :] = y[8:]

    def gather_group(g):
        for t in range(QUARTERS):
            for h in range(2):
                base = (16 * g + 8 * h) * 8 + 4 * (t % 2)
                p = [prod[t // 2, pl.ds(base + s, 8, stride=8), :] for s in range(SUBJ_DEV)]
                sums[4 * g + t, pl.ds(8 * h, 8), :] = (p[0] + p[1]) + (p[2] + p[3])

    def rs_copy(owner, src):
        return pltpu.make_async_remote_copy(
            src_ref=sums.at[owner], dst_ref=got.at[src], send_sem=rs_send.at[owner],
            recv_sem=rs_recv.at[src], device_id=(owner, slab), device_id_type=MESH)

    def dn_copy(owner, src):
        return pltpu.make_async_remote_copy(
            src_ref=den.at[me], dst_ref=den.at[src], send_sem=dn_send.at[owner],
            recv_sem=dn_recv.at[src], device_id=(owner, slab), device_id_type=MESH)

    def send_group(g):
        def one(t, _):
            owner = 4 * g + lax.rem(t + me, 4)

            @pl.when(owner != me)
            def _():
                rs_copy(owner, me).start()

            return 0

        lax.fori_loop(0, QUARTERS, one, 0)

    prod[:, COEF * 8:, :] = jnp.zeros((2, 3 * 8, LANES), jnp.float32)

    def map_copy(k):
        peer = lax.rem(slab + k, n_slab)
        return pltpu.make_async_remote_copy(
            src_ref=maps.at[slab], dst_ref=maps.at[slab], send_sem=mp_send.at[k],
            recv_sem=mp_recv.at[slab], device_id=(me, peer), device_id_type=MESH)

    def map_wait(src):
        return pltpu.make_async_remote_copy(
            src_ref=maps.at[src], dst_ref=maps.at[src], send_sem=mp_send.at[0],
            recv_sem=mp_recv.at[src], device_id=(me, sib), device_id_type=MESH)

    for i, (c0, n, cp) in enumerate(chunks):
        cp.wait()
        compute(c0, n)
        if i == 1:
            gather_group(0)
            pl.semaphore_wait(barrier, n_subj - 1 + n_slab - 1)

            def send_dn(k, _):
                owner = lax.rem(me + k, n_subj)

                @pl.when(owner < OWNERS)
                def _():
                    dn_copy(owner, me).start()

                return 0

            lax.fori_loop(1, n_subj, send_dn, 0)
            send_group(0)

            def send_map(k, _):
                map_copy(k).start()
                return 0

            lax.fori_loop(1, n_slab, send_map, 0)
        if i == 3:
            gather_group(1)
            send_group(1)
    gather_group(2)
    send_group(2)

    def tile_copy(dst):
        return pltpu.make_async_remote_copy(
            src_ref=slabs.at[slab, me], dst_ref=slabs.at[slab, me], send_sem=ag_send.at[dst],
            recv_sem=ag_recv.at[me], device_id=(dst, slab), device_id_type=MESH)

    def tile_wait(owner):
        return pltpu.make_async_remote_copy(
            src_ref=slabs.at[slab, owner], dst_ref=slabs.at[slab, owner], send_sem=ag_send.at[owner],
            recv_sem=ag_recv.at[owner], device_id=(owner, slab), device_id_type=MESH)

    @pl.when(me < OWNERS)
    def _():
        t = lax.rem(me, QUARTERS)

        def add_den(k, total):
            src = lax.rem(me + k, n_subj)
            dn_copy(0, src).wait_recv()
            return total + den[src]

        total_den = lax.fori_loop(1, n_subj, add_den, den[me])
        quarter = lax.broadcasted_iota(jnp.int32, (QUARTERS, LANES), 0)
        mine = jnp.sum(jnp.where(quarter == t, total_den, 0.0), axis=0, keepdims=True)

        def add(k, total):
            src = lax.rem(me + k, n_subj)
            rs_copy(0, src).wait_recv()
            return total + got[src]

        total = lax.fori_loop(1, n_subj, add, sums[me])
        slabs[slab, me] = (total / mine).astype(jnp.bfloat16)

        def send(k, _):
            tile_copy(lax.rem(me + k, n_subj)).start()
            return 0

        lax.fori_loop(1, n_subj, send, 0)

    def await_tile(k, _):
        owner = lax.rem(me + k, n_subj)

        @pl.when(owner < OWNERS)
        def _():
            tile_wait(owner).wait_recv()

        return 0

    lax.fori_loop(1, n_subj, await_tile, 0)

    chips = n_slab // 2

    def slab_copy(q, dst, send_sem, recv_sem):
        return pltpu.make_async_remote_copy(
            src_ref=slabs.at[q], dst_ref=slabs.at[q], send_sem=send_sem, recv_sem=recv_sem,
            device_id=(me, dst), device_id_type=MESH)

    def partner(k):
        return lax.rem(slab // 2 + k, chips) * 2 + core

    def send_slab(k, _):
        slab_copy(slab, partner(k), sl_send.at[k], sl_recv.at[slab]).start()
        return 0

    lax.fori_loop(1, chips, send_slab, 0)
    slab_copy(slab, sib, sib_send.at[0], sib_recv.at[slab]).start()

    def expand(q):
        base = pl.multiple_of(q * (BLOCKS * LANES), BLOCKS * LANES)
        for b in range(BLOCKS):
            ranks = jnp.broadcast_to(maps[q, pl.ds(b, 1), :], (8, LANES))
            source = ranks // LANES
            lane = ranks - source * LANES
            lane = jnp.where(ranks < 0, 0, lane)
            low, high = max(0, b - 4), min(b, 3)
            for g in range(GROUPS):
                tiles = [slabs[q, 4 * g + t].astype(jnp.float32) for t in range(low, high + 1)]
                halves = []
                for h in range(2):
                    value = jnp.zeros((8, LANES), jnp.float32)
                    for t, tile in zip(range(low, high + 1), tiles):
                        picked = jnp.take_along_axis(tile[8 * h:8 * h + 8], lane, axis=1)
                        value = jnp.where((ranks >= 0) & (source == t), picked, value)
                    halves.append(value)
                both = jnp.concatenate(halves, axis=0).astype(jnp.bfloat16)
                rows = min(16, COEF - 16 * g)
                out_ref[pl.ds(16 * g, rows), pl.ds(pl.multiple_of(base + b * LANES, LANES), LANES)] = both[:rows]

    def await_maps(k, _):
        map_wait(lax.rem(slab + k, n_slab)).wait_recv()
        return 0

    lax.fori_loop(1, n_slab, await_maps, 0)

    def visit(k, _):
        @pl.when((k > 0) & (k < chips))
        def _():
            q = partner(chips - k)
            slab_copy(q, sib, sl_send.at[0], sl_recv.at[q]).wait_recv()
            slab_copy(q, sib, sib_send.at[k], sib_recv.at[q]).start()

        @pl.when(k >= chips)
        def _():
            q = lax.rem(sib // 2 + 2 * chips - k, chips) * 2 + lax.rem(sib, 2)
            slab_copy(q, sib, sib_send.at[0], sib_recv.at[q]).wait_recv()

        q = lax.rem(slab // 2 + 2 * chips - k, chips) * 2 + jnp.where(k < chips, core, 1 - core)
        expand(q)
        return 0

    lax.fori_loop(0, 2 * chips, visit, 0)

    def drain_slab(k, _):
        slab_copy(slab, partner(k), sl_send.at[k], sl_recv.at[slab]).wait_send()
        return 0

    lax.fori_loop(1, chips, drain_slab, 0)

    def drain_sib(k, _):
        slab_copy(slab, sib, sib_send.at[k], sib_recv.at[slab]).wait_send()
        return 0

    lax.fori_loop(0, chips, drain_sib, 0)

    def drain_map(k, _):
        map_copy(k).wait_send()
        return 0

    lax.fori_loop(1, n_slab, drain_map, 0)

    def drain_subj(k, _):
        peer = lax.rem(me + k, n_subj)

        @pl.when(peer < OWNERS)
        def _():
            rs_copy(peer, me).wait_send()
            dn_copy(peer, me).wait_send()

        @pl.when(me < OWNERS)
        def _():
            tile_copy(peer).wait_send()

        return 0

    lax.fori_loop(1, n_subj, drain_subj, 0)


def on_device(n_subj, n_slab, fod, rotation, modulation, subject_ids, subject_weight, voxel_cell_index):
    rot = rotation.reshape(SUBJ_DEV, COEF, COEF, QUARTERS, LANES).transpose(1, 2, 3, 0, 4).reshape(COEF, COEF, 16, LANES)
    fo = fod.reshape(SUBJ_DEV, COEF, QUARTERS, LANES).transpose(1, 2, 0, 3).reshape(COEF, 16, LANES)
    mod = modulation.reshape(SUBJ_DEV, QUARTERS, LANES).transpose(1, 0, 2).reshape(16, LANES)
    cells = voxel_cell_index.reshape(1, QUARTERS * LANES)
    n_chunks = -(-COEF // CHUNK)
    dma = pltpu.SemaphoreType.DMA
    hbm = pl.BlockSpec(memory_space=pltpu.HBM)
    smem = pl.BlockSpec(memory_space=pltpu.SMEM)
    chips = n_slab // 2
    return pl.pallas_call(
        functools.partial(kernel, n_subj, n_slab),
        out_shape=jax.ShapeDtypeStruct((COEF, n_slab * BLOCKS * LANES), jnp.bfloat16),
        in_specs=[hbm, hbm, hbm, hbm, smem, smem],
        out_specs=pl.BlockSpec(memory_space=pltpu.VMEM),
        scratch_shapes=[
            pltpu.VMEM((COEF, COEF, 16, LANES), jnp.bfloat16),
            pltpu.VMEM((COEF, 16, LANES), jnp.bfloat16),
            pltpu.VMEM((COEF, 16, LANES), jnp.float32),
            pltpu.VMEM((16, LANES), jnp.float32),
            pltpu.VMEM((1, QUARTERS * LANES), jnp.int32),
            pltpu.VMEM((2, 48 * 8, LANES), jnp.float32),
            pltpu.VMEM((OWNERS, 16, LANES), jnp.float32),
            pltpu.VMEM((n_subj, 16, LANES), jnp.float32),
            pltpu.VMEM((n_subj, QUARTERS, LANES), jnp.float32),
            pltpu.VMEM((n_slab, OWNERS, 16, LANES), jnp.bfloat16),
            pltpu.VMEM((n_slab, BLOCKS, LANES), jnp.int32),
            dma((n_chunks,)), dma((3,)),
            dma((n_subj,)), dma((n_subj,)), dma((n_subj,)), dma((n_subj,)),
            dma((n_subj,)), dma((n_subj,)),
            dma((chips,)), dma((n_slab,)), dma((chips,)), dma((n_slab,)),
            dma((n_slab,)), dma((n_slab,)),
        ],
        compiler_params=pltpu.CompilerParams(
            collective_id=0, has_side_effects=True, vmem_limit_bytes=60 * 1024 * 1024),
    )(rot, fo, mod, cells, subject_ids, subject_weight)


def solution(mesh):
    placed = (
        P("subj", None, "slab"),
        P("subj", None, None, "slab"),
        P("subj", "slab"),
        P("subj"),
        P(),
        P("slab"),
    )
    body = functools.partial(on_device, mesh.shape["subj"], mesh.shape["slab"])
    return jax.shard_map(body, mesh=mesh, in_specs=placed, out_specs=P(), check_vma=False)
```

time: 93 us -> 37.5 us (0.40)
  Pallas kernels: 0 us -> 34.7 us
  blocking collectives: 29 us -> 0 us
  starting transfers between devices: 24.3 us -> 0 us
  waiting for transfers between devices: 17.7 us -> 0 us
  other arithmetic: 10.8 us -> 0 us
  local copies, waits for them, and re-layouts: 9.83 us -> 2.65 us
    pallas_call x0 -> x1, Pallas kernels: none -> 34.7 us  [on_device(): pl.pallas_call(functools.partial(kernel, n_subj, n_slab), out_shape=jax.S...]
    all_to_all x1 -> x0, blocking collectives: 29 us -> none  [from_everyone(): return lax.all_to_all(copies, axis, split_axis=0, concat_axis=0, tiled=True)]
    all_to_all x3 -> x0, starting transfers between devices: 24.3 us -> none  [the longest x2 20.8 us: sum_at_owner(): lax.all_to_all(blocks, axis, split_axis=0, concat_axis=0, tiled=True)]
    all_to_all x3 -> x0, waiting for transfers between devices: 17.7 us -> none  [the longest x2 8.89 us: sum_at_owner(): lax.all_to_all(blocks, axis, split_axis=0, concat_axis=0, tiled=True)]
    dot_general x1 -> x0, other arithmetic: 7.78 us -> none  [on_device(): jnp.einsum('xfhu,xhu->xfu', rotation, fod, preferred_element_type=jnp.flo...]
    unnamed x11 -> x1, local copies, waits for them, and re-layouts: 5.26 us -> 2.65 us
    scatter x2 -> x0, local copies, waits for them, and re-layouts: 1.99 us -> none  [on_device(): dense = dense.at[:, voxel_cell_index].set(average)]
    all_to_all x2 -> x0, local copies, waits for them, and re-layouts: 1.19 us -> none  [sum_at_owner(): lax.all_to_all(blocks, axis, split_axis=0, concat_axis=0, tiled=True)]
  transfers between devices with their start and end apart: 3 -> 0, of which waited for: 2 -> 0; matrix products, arithmetic and copies ran while one was open for 11% -> 0% of each run, Pallas kernels for 0% -> 0%
where the time goes in v1:
time: 37.5 us; the launch traced here: 37.4 us
  Pallas kernels  34.7 us (93%)
  local copies, waits for them, and re-layouts  2.65 us (7%)
    pallas_call x1, Pallas kernels, on_device(): pl.pallas_call(functools.partial(kernel, n_subj, n_slab), out_shape=jax.S...  34.7 us
    unnamed x1, local copies, waits for them, and re-layouts  2.65 us

profile of v1, /device:TPU:1, one launch (start us, length us, event | category | flops | bytes accessed | tf_op | source)
XLA Modules:
  0.0 37.4 jit_solution(12121897794234662058)
XLA Ops:
  0.0 34.7 %shard_map.64 = bf16[45,16384]{1,0:T(8,128)(2,1)} custom-call(bf16[45,45,16,128]{3,2,1,0:T(8,128)(2,1)} %bitcast.16, bf16[45,16,128]{2,1,0:T(8,128)(2,1)} %bitcast.17, f32[16,128]{1,0:T(8,128)} %bitcast.18, s32[1,512]{1,0:T(1,128)} %bitcast.19, s32[4]{0:T(128)} %ids_ref.1, f32[64]{0:T(128)} %sw_ref.1), custom_call_target="tpu_custom_call" | custom-call | tf_op jit(solution)/shard_map/pallas_call | solution.py:330
  34.7 2.7 %copy.11 = bf16[45,16384]{1,0:T(8,128)(2,1)} copy(bf16[45,16384]{1,0:T(8,128)(2,1)} %shard_map.64) | data formatting | bytes 2949120
